TPU v7x, 32 devices: a whole 2x2x4 slice. The times are simulated.
32 devices in a mesh: dp: 16 (over z, y, core), mlp: 2 (over x).
Axes of the slice: x: 2, y: 2, z: 4, core: 2. Of those that a mesh axis runs over, the one named last changes fastest.
Arguments:
- block_input: bfloat16 [16, 2, 160, 1024], P('dp', 'mlp'), may hold values from -6 to 6
- span_offset: int32 [16, 2], replicated, may hold values from 0 to 15, as said below
- ln_gain: float32 [1024], replicated, may hold values from 0.5 to 1.5
- ln_bias: float32 [1024], replicated, may hold values from -3 to 3
- w_qkv: bfloat16 [1024, 3072], replicated, may hold values from -0.25 to 0.25
- b_qkv: float32 [3072], replicated, may hold values from -3 to 3
- w_out: bfloat16 [1024, 1024], replicated, may hold values from -1 to 1
- b_out: float32 [1024], replicated, may hold values from -3 to 3
- w_up: bfloat16 [1024, 4096], P(None, 'mlp'), may hold values from -0.1875 to 0.1875
- b_up: float32 [4096], P('mlp'), may hold values from -3 to 3
- w_down: bfloat16 [4096, 1024], P('mlp'), may hold values from -0.09375 to 0.09375
- b_down: float32 [1024], replicated, may hold values from -3 to 3
- cotangent: bfloat16 [16, 2, 160, 1024], P('dp', 'mlp'), may hold values from -6 to 6
Outputs:
- output: bfloat16 [16, 2, 160, 1024], P('dp', 'mlp')
- grad_input: float32 [16, 2, 160, 1024], P('dp', 'mlp')
- grad_ln_gain: float32 [1024], P('mlp')
- grad_ln_bias: float32 [1024], P('mlp')
- grad_w_qkv: float32 [1024, 3072], P(None, 'mlp')
- grad_b_qkv: float32 [3072], P('mlp')
- grad_w_out: float32 [1024, 1024], P(None, 'mlp')
- grad_b_out: float32 [1024], P('mlp')
- grad_w_up: float32 [1024, 4096], P(None, 'mlp')
- grad_b_up: float32 [4096], P('mlp')
- grad_w_down: float32 [4096, 1024], P('mlp')
- grad_b_down: float32 [1024], P('mlp')
Inputs may be any that keep to these rules, and one draw needn't show every extreme that they name: For every sequence s, span_offset[:, s] is a permutation of 0 to 15.
All inputs are finite; a program needn't handle non-finite values.
Results may differ from a plain program's by a relative error of at most 0.02.
Values may be sent and summed in bfloat16 or wider, within the bound.
A program may use at most 256 MiB of HBM per device.

v0:
```python
import math
import jax
import jax.numpy as jnp
from jax import lax
from jax.sharding import PartitionSpec as P

HEADS = 16
HEAD_DIM = 64
ROT = 16
EPSILON = 1e-05
ROPE_BASE = 10000.0
SQRT_HALF = 1.0 / math.sqrt(2.0)
INV_ROOT_TWO_PI = 1.0 / math.sqrt(2.0 * math.pi)


def rotate(values, positions, sign_factor):
    half_rot = ROT // 2
    frequency = ROPE_BASE ** (-(jnp.arange(half_rot, dtype=jnp.float32) * 2.0 / ROT))
    angles = positions.astype(jnp.float32)[:, None] * frequency[None, :]
    cosine = jnp.cos(angles)[:, None, :]
    sine_part = sign_factor * jnp.sin(angles)[:, None, :]
    first_half = values[..., :half_rot]
    second_half = values[..., half_rot:ROT]
    return jnp.concatenate(
        [
            first_half * cosine - second_half * sine_part,
            second_half * cosine + first_half * sine_part,
            values[..., ROT:],
        ],
        axis=-1,
    )


def gelu_exact(values):
    return 0.5 * values * (1.0 + lax.erf(values * SQRT_HALF))


def gelu_slope(values):
    return (
        0.5 * (1.0 + lax.erf(values * SQRT_HALF))
        + values * jnp.exp(-0.5 * values * values) * INV_ROOT_TWO_PI
    )


def piece_count(total_rows):
    count_blocks = max(1, total_rows // 1024)
    while total_rows % count_blocks:
        count_blocks += 1
    return count_blocks


def row_positions(offsets, count_rows, tok_count):
    index_all = jnp.arange(count_rows, dtype=jnp.int32)
    span_of = index_all // tok_count
    within = index_all - span_of * tok_count
    matches = span_of[:, None] == jnp.arange(offsets.shape[0], dtype=jnp.int32)[None, :]
    offset_of = jnp.sum(jnp.where(matches, offsets[None, :], 0), axis=1)
    return offset_of * tok_count + within


def contract_rows(left_mat, right_mat):
    return lax.dot_general(
        left_mat, right_mat, (((0,), (0,)), ((), ())), preferred_element_type=jnp.float32
    )


def contract_cols(left_mat, right_mat):
    return lax.dot_general(
        left_mat, right_mat, (((1,), (1,)), ((), ())), preferred_element_type=jnp.float32
    )


def local(
    block_input,
    span_offset,
    ln_gain,
    ln_bias,
    w_qkv,
    b_qkv,
    w_out,
    b_out,
    w_up,
    b_up,
    w_down,
    b_down,
    cotangent,
):
    tok_count = block_input.shape[2]
    model_width = block_input.shape[3]
    scale_dot = 1.0 / math.sqrt(HEAD_DIM)
    span_here = lax.axis_index("dp")
    seq_here = lax.axis_index("mlp")
    offsets = lax.dynamic_index_in_dim(span_offset, seq_here, axis=1, keepdims=False)
    offset_here = lax.dynamic_index_in_dim(offsets, span_here, axis=0, keepdims=False)
    positions = offset_here * tok_count + jnp.arange(tok_count, dtype=jnp.int32)
    row_data = block_input[0, 0].astype(jnp.float32)
    centre = jnp.mean(row_data, axis=-1, keepdims=True)
    centred = row_data - centre
    spread = jnp.mean(centred * centred, axis=-1, keepdims=True)
    inv_scale = lax.rsqrt(spread + EPSILON)
    unit_rows = centred * inv_scale
    normed = (unit_rows * ln_gain + ln_bias).astype(jnp.bfloat16)
    project = jnp.dot(normed, w_qkv, preferred_element_type=jnp.float32) + b_qkv
    queries = rotate(
        project[:, :model_width].reshape(tok_count, HEADS, HEAD_DIM), positions, 1.0
    ).astype(jnp.bfloat16)
    keys_here = rotate(
        project[:, model_width : 2 * model_width].reshape(tok_count, HEADS, HEAD_DIM),
        positions,
        1.0,
    ).astype(jnp.bfloat16)
    values_here = (
        project[:, 2 * model_width :].reshape(tok_count, HEADS, HEAD_DIM).astype(jnp.bfloat16)
    )
    keys_flat = keys_here.reshape(tok_count, model_width)
    values_flat = values_here.reshape(tok_count, model_width)
    start_state = (
        jnp.zeros((tok_count, HEADS, HEAD_DIM), jnp.float32),
        jnp.zeros((HEADS, tok_count), jnp.float32),
    )
    keys_piece = lax.all_gather(keys_flat, "dp", axis=0, tiled=True)
    values_piece = lax.all_gather(values_flat, "dp", axis=0, tiled=True)
    piece_rows = keys_piece.shape[0]
    blocks = piece_count(piece_rows)
    sub_rows = piece_rows // blocks
    key_pos = row_positions(offsets, piece_rows, tok_count)

    def attend_one_block(state_now, packed):
        keys_blk, values_blk, pos_blk = packed
        key_heads = keys_blk.reshape(sub_rows, HEADS, HEAD_DIM)
        value_heads = values_blk.reshape(sub_rows, HEADS, HEAD_DIM)
        scores = (
            jnp.einsum("qhd,khd->hqk", queries, key_heads, preferred_element_type=jnp.float32)
            * scale_dot
        )
        allowed = pos_blk[None, :] <= positions[:, None]
        weights_exp = jnp.where(allowed[None], jnp.exp(scores), 0.0)
        mixed_sum, totals = state_now
        mixed_sum = mixed_sum + jnp.einsum(
            "hqk,khd->qhd",
            weights_exp.astype(jnp.bfloat16),
            value_heads,
            preferred_element_type=jnp.float32,
        )
        return ((mixed_sum, totals + jnp.sum(weights_exp, axis=-1)), None)

    state_now, _unused = lax.scan(
        attend_one_block,
        start_state,
        (
            keys_piece.reshape(blocks, sub_rows, model_width),
            values_piece.reshape(blocks, sub_rows, model_width),
            key_pos.reshape(blocks, sub_rows),
        ),
    )
    mixed_sum, totals = state_now
    attended = mixed_sum / totals.T[:, :, None]
    attended_low = attended.reshape(tok_count, model_width).astype(jnp.bfloat16)
    attn_branch = jnp.dot(attended_low, w_out, preferred_element_type=jnp.float32) + b_out
    normed_all = lax.all_gather(normed, "mlp", axis=0, tiled=True)
    up_proj = jnp.dot(normed_all, w_up, preferred_element_type=jnp.float32) + b_up
    activated = gelu_exact(up_proj).astype(jnp.bfloat16)
    mlp_branch = (
        lax.psum_scatter(
            jnp.dot(activated, w_down, preferred_element_type=jnp.float32).astype(jnp.bfloat16),
            "mlp",
            scatter_dimension=0,
            tiled=True,
        ).astype(jnp.float32)
        + b_down
    )
    output = (row_data + attn_branch + mlp_branch).astype(jnp.bfloat16)
    grad_out = cotangent[0, 0]
    grad_w_out = contract_rows(attended_low, grad_out)
    grad_bias_out = jnp.sum(grad_out.astype(jnp.float32), axis=0)
    grad_all = lax.all_gather(grad_out, "mlp", axis=0, tiled=True)
    grad_w_down = contract_rows(activated, grad_all)
    grad_act = contract_cols(grad_all, w_down)
    grad_up = (grad_act * gelu_slope(up_proj)).astype(jnp.bfloat16)
    grad_w_up = contract_rows(normed_all, grad_up)
    grad_b_up = jnp.sum(grad_up.astype(jnp.float32), axis=0)
    grad_norm_mlp = lax.psum_scatter(
        contract_cols(grad_up, w_up).astype(jnp.bfloat16), "mlp", scatter_dimension=0, tiled=True
    ).astype(jnp.float32)
    grad_att = contract_cols(grad_out, w_out).reshape(tok_count, HEADS, HEAD_DIM)
    grad_mixed = (grad_att / totals.T[:, :, None]).astype(jnp.bfloat16)
    grad_totals = ((-jnp.sum(grad_att * attended, axis=-1)).T / totals).astype(jnp.bfloat16)
    grad_totals_wide = grad_totals.astype(jnp.float32)[:, :, None]
    zero_heads = jnp.zeros((tok_count, HEADS, HEAD_DIM), jnp.float32)
    grad_query_sum = zero_heads
    keys_piece = lax.all_gather(keys_flat, "dp", axis=0, tiled=True)
    values_piece = lax.all_gather(values_flat, "dp", axis=0, tiled=True)
    piece_rows = keys_piece.shape[0]
    blocks = piece_count(piece_rows)
    back_sub_rows = piece_rows // blocks
    key_pos = row_positions(offsets, piece_rows, tok_count)

    def back_one_block(running_sum, packed):
        keys_blk, values_blk, pos_blk = packed
        key_heads = keys_blk.reshape(back_sub_rows, HEADS, HEAD_DIM)
        value_heads = values_blk.reshape(back_sub_rows, HEADS, HEAD_DIM)
        scores = (
            jnp.einsum("qhd,khd->hqk", queries, key_heads, preferred_element_type=jnp.float32)
            * scale_dot
        )
        allowed = pos_blk[None, :] <= positions[:, None]
        weights_exp = jnp.where(allowed[None], jnp.exp(scores), 0.0)
        grad_exp = jnp.einsum(
            "qhd,khd->hqk", grad_mixed, value_heads, preferred_element_type=jnp.float32
        )
        grad_scores = (weights_exp * (grad_exp + grad_totals_wide)).astype(jnp.bfloat16)
        running_sum = running_sum + scale_dot * jnp.einsum(
            "hqk,khd->qhd", grad_scores, key_heads, preferred_element_type=jnp.float32
        )
        grad_key_blk = scale_dot * jnp.einsum(
            "hqk,qhd->khd", grad_scores, queries, preferred_element_type=jnp.float32
        )
        grad_value_blk = jnp.einsum(
            "hqk,qhd->khd",
            weights_exp.astype(jnp.bfloat16),
            grad_mixed,
            preferred_element_type=jnp.float32,
        )
        joined = jnp.concatenate(
            [
                grad_key_blk.reshape(back_sub_rows, model_width),
                grad_value_blk.reshape(back_sub_rows, model_width),
            ],
            axis=1,
        )
        return (running_sum, joined)

    grad_query_sum, stacked = lax.scan(
        back_one_block,
        grad_query_sum,
        (
            keys_piece.reshape(blocks, back_sub_rows, model_width),
            values_piece.reshape(blocks, back_sub_rows, model_width),
            key_pos.reshape(blocks, back_sub_rows),
        ),
    )
    grad_kv_sum = stacked.reshape(piece_rows, 2 * model_width)
    grad_kv = lax.psum_scatter(
        grad_kv_sum.astype(jnp.bfloat16), "dp", scatter_dimension=0, tiled=True
    ).astype(jnp.float32)
    grad_keys = grad_kv[:, :model_width].reshape(tok_count, HEADS, HEAD_DIM)
    grad_values = grad_kv[:, model_width:].reshape(tok_count, HEADS, HEAD_DIM)
    grad_query_pre = rotate(grad_query_sum, positions, -1.0).reshape(tok_count, model_width)
    grad_key_pre = rotate(grad_keys, positions, -1.0).reshape(tok_count, model_width)
    grad_project = jnp.concatenate(
        [grad_query_pre, grad_key_pre, grad_values.reshape(tok_count, model_width)], axis=1
    ).astype(jnp.bfloat16)
    grad_w_qkv = contract_rows(normed, grad_project)
    grad_b_qkv = jnp.sum(grad_project.astype(jnp.float32), axis=0)
    grad_normed = contract_cols(grad_project, w_qkv) + grad_norm_mlp
    grad_ln_gain = jnp.sum(grad_normed * unit_rows, axis=0)
    grad_ln_bias = jnp.sum(grad_normed, axis=0)
    grad_unit = grad_normed * ln_gain
    grad_rows = inv_scale * (
        grad_unit
        - jnp.mean(grad_unit, axis=-1, keepdims=True)
        - unit_rows * jnp.mean(grad_unit * unit_rows, axis=-1, keepdims=True)
    )
    grad_input = (grad_out.astype(jnp.float32) + grad_rows).reshape(1, 1, tok_count, model_width)
    part_qkv, part_out, part_bqkv, part_bias, part_gain, part_shift = (
        lax.psum_scatter(
            grad_w_qkv.astype(jnp.bfloat16), "mlp", scatter_dimension=1, tiled=True
        ).astype(jnp.float32),
        lax.psum_scatter(
            grad_w_out.astype(jnp.bfloat16), "mlp", scatter_dimension=1, tiled=True
        ).astype(jnp.float32),
        lax.psum_scatter(
            grad_b_qkv.astype(jnp.bfloat16), "mlp", scatter_dimension=0, tiled=True
        ).astype(jnp.float32),
        lax.psum_scatter(
            grad_bias_out.astype(jnp.bfloat16), "mlp", scatter_dimension=0, tiled=True
        ).astype(jnp.float32),
        lax.psum_scatter(
            grad_ln_gain.astype(jnp.bfloat16), "mlp", scatter_dimension=0, tiled=True
        ).astype(jnp.float32),
        lax.psum_scatter(
            grad_ln_bias.astype(jnp.bfloat16), "mlp", scatter_dimension=0, tiled=True
        ).astype(jnp.float32),
    )
    summed = (
        lax.psum(part_qkv.astype(jnp.bfloat16), "dp").astype(jnp.float32),
        lax.psum(part_out.astype(jnp.bfloat16), "dp").astype(jnp.float32),
        lax.psum(part_bqkv.astype(jnp.bfloat16), "dp").astype(jnp.float32),
        lax.psum(part_bias.astype(jnp.bfloat16), "dp").astype(jnp.float32),
        lax.psum(part_gain.astype(jnp.bfloat16), "dp").astype(jnp.float32),
        lax.psum(part_shift.astype(jnp.bfloat16), "dp").astype(jnp.float32),
        lax.psum(grad_w_up.astype(jnp.bfloat16), "dp").astype(jnp.float32),
        lax.psum(grad_b_up.astype(jnp.bfloat16), "dp").astype(jnp.float32),
        lax.psum(grad_w_down.astype(jnp.bfloat16), "dp").astype(jnp.float32),
    )
    return (
        output.reshape(1, 1, tok_count, model_width),
        grad_input,
        summed[4],
        summed[5],
        summed[0],
        summed[2],
        summed[1],
        summed[3],
        summed[6],
        summed[7],
        summed[8],
        summed[3],
    )


def solution(mesh):
    return jax.shard_map(
        local,
        mesh=mesh,
        in_specs=(
            P("dp", "mlp", None, None),
            P(),
            P(),
            P(),
            P(),
            P(),
            P(),
            P(),
            P(None, "mlp"),
            P("mlp"),
            P("mlp", None),
            P(),
            P("dp", "mlp", None, None),
        ),
        out_specs=(
            P("dp", "mlp", None, None),
            P("dp", "mlp", None, None),
            P("mlp"),
            P("mlp"),
            P(None, "mlp"),
            P("mlp"),
            P(None, "mlp"),
            P("mlp"),
            P(None, "mlp"),
            P("mlp"),
            P("mlp", None),
            P("mlp"),
        ),
        check_vma=False,
    )
```

profile of v0, /device:TPU:0, one launch (start us, length us, event | category | flops | bytes accessed | tf_op | source)
XLA Modules:
  0.0 848.6 jit_solution(7495591158141131622)
XLA Ops:
  15.1 4.1 convolution_add_fusion
  38.3 52.1 %all-gather.6.cloned.1.call-done = bf16[2560,1024]{1,0:T(8,128)(2,1)} async-done(((bf16[160,1024]{1,0:T(8,128)(2,1)}), bf16[2560,1024]{1,0:T(8,128)(2,1)}) %all-gather.6.cloned.1.call-update) | async-done | bytes 5242896 | tf_op jit(solution)/shard_map/all_gather | solution.py:121
  90.4 7.9 copy.85
  98.3 49.4 %all-gather.4.cloned.1.call-done = bf16[2560,1024]{1,0:T(8,128)(2,1)} async-done(((bf16[160,1024]{1,0:T(8,128)(2,1)}), bf16[2560,1024]{1,0:T(8,128)(2,1)}) %all-gather.4.cloned.1.call-update) | async-done | bytes 5242896 | tf_op jit(solution)/shard_map/all_gather | solution.py:122
  147.7 7.9 copy.84
  155.5 40.2 %while.26 = (s32[]{:T(128)}, f32[160,16,64]{0,2,1:T(8,128)}, f32[16,160]{1,0:T(8,128)S(1)}, bf16[2,1280,1024]{1,2,0:T(8,128)(2,1)}, s32[2,1280]{1,0:T(2,128)S(1)...) while((s32[]{:T(128)}, f32[160,16,64]{0,2,1:T(8,128)}, ...), condition=%wide.region_5.6_spmd.clone, body=%wide.region_3.5_spmd.clone.sunk | while | flops 859056768 | bytes 44253560 | solution.py:147
  155.5 4.4 constant_dynamic-slice_fusion.6
  160.1 6.5 fusion.124
  166.7 8.9 %fusion.125 = f32[160,16,64]{0,2,1:T(8,128)} fusion(bf16[1280,16,64]{0,2,1:T(8,128)(2,1)} %bitcast.209, f32[16,1280,160]{1,2,0:T(8,128)} %get-tuple-element.480, pred[160,1280]{1,0:T(8,128)(4,1)S(1)} %broadcast_compare_fusion.4, f32[160,16,64]{0,2,1:T(8,128)} %get-tuple-element.505, pred[]{:T(512)S(6)} %compare.6), kind=kOutput, calls=%fused_computation.10.clone.1 | convolution fusion | flops 429588480 | bytes 17244160 | tf_op jit(solution)/shard_map/while/body/eval_jaxpr/hqk,khd->qhd/dot_general | solution.py:139
  175.5 4.4 constant_dynamic-slice_fusion.6
  180.1 6.5 fusion.124
  186.7 9.1 %fusion.125 = f32[160,16,64]{0,2,1:T(8,128)} fusion(bf16[1280,16,64]{0,2,1:T(8,128)(2,1)} %bitcast.209, f32[16,1280,160]{1,2,0:T(8,128)} %get-tuple-element.480, pred[160,1280]{1,0:T(8,128)(4,1)S(1)} %broadcast_compare_fusion.4, f32[160,16,64]{0,2,1:T(8,128)} %get-tuple-element.505, pred[]{:T(512)S(6)} %compare.6), kind=kOutput, calls=%fused_computation.10.clone.1 | convolution fusion | flops 429588480 | bytes 17244160 | tf_op jit(solution)/shard_map/while/body/eval_jaxpr/hqk,khd->qhd/dot_general | solution.py:139
  198.7 110.8 %while.27 = (s32[]{:T(128)}, f32[160,16,64]{0,2,1:T(8,128)}, bf16[2,1280,2048]{2,1,0:T(8,128)(2,1)}, bf16[2,1280,1024]{1,2,0:T(8,128)(2,1)}, s32[2,1280]{1,0:T(2...) while((s32[]{:T(128)}, f32[160,16,64]{0,2,1:T(8,128)}, ...), condition=%wide.region_9.10_spmd.clone, body=%wide.region_8.9_spmd.clone.sunk | while | flops 2137170048 | bytes 206425072 | solution.py:233
  198.9 4.4 constant_dynamic-slice_fusion.7
  203.2 6.6 fusion.136
  210.1 9.9 %fusion.137 = bf16[16,160,1280]{2,1,0:T(8,128)(2,1)S(1)} fusion(f32[16,1280,160]{1,2,0:T(8,128)} %fusion.136, bf16[1280,16,64]{0,2,1:T(8,128)(2,1)} %bitcast.211, bf16[160,16,64]{0,2,1:T(8,128)(2,1)} %get-tuple-element.555, f32[16,160]{1,0:T(8,128)S(1)} %bitcast.219, pred[160,1280]{1,0:T(8,128)(4,1)S(1)} %broadcast_compare_fusion.5), kind=kOutput, calls=%fused_computation.20.clone.1 | convolution fusion | flops 435814400 | bytes 22824960 | tf_op jit(solution)/shard_map/while/body/eval_jaxpr/qhd,khd->hqk/dot_general | solution.py:208
  223.4 3.8 copy-done.2
  227.1 3.7 fusion.139
  233.6 8.0 copy.108
  241.5 5.6 constant_dynamic-update-slice_fusion.2
  247.1 6.9 fusion.138
  254.0 4.4 constant_dynamic-slice_fusion.7
  258.4 6.6 fusion.136
  265.2 9.9 %fusion.137 = bf16[16,160,1280]{2,1,0:T(8,128)(2,1)S(1)} fusion(f32[16,1280,160]{1,2,0:T(8,128)} %fusion.136, bf16[1280,16,64]{0,2,1:T(8,128)(2,1)} %bitcast.211, bf16[160,16,64]{0,2,1:T(8,128)(2,1)} %get-tuple-element.555, f32[16,160]{1,0:T(8,128)S(1)} %bitcast.219, pred[160,1280]{1,0:T(8,128)(4,1)S(1)} %broadcast_compare_fusion.5), kind=kOutput, calls=%fused_computation.20.clone.1 | convolution fusion | flops 435814400 | bytes 22824960 | tf_op jit(solution)/shard_map/while/body/eval_jaxpr/qhd,khd->hqk/dot_general | solution.py:208
  278.5 3.8 copy-done.2
  282.3 3.7 fusion.139
  288.7 8.0 copy.108
  296.7 5.7 constant_dynamic-update-slice_fusion.2
  302.4 7.1 fusion.138
  317.7 3.5 multiply_subtract_fusion
  326.5 101.3 %reduce-scatter.8.cloned.1.call-done = bf16[160,2048]{1,0:T(8,128)(2,1)} async-done(((bf16[2560,2048]{1,0:T(8,128)(2,1)}), bf16[160,2048]{1,0:T(8,128)(2,1)}) %reduce-scatter.8.cloned.1.call-update) | async-done | bytes 655376 | tf_op jit(solution)/shard_map/reduce_scatter | solution.py:243
  436.3 5.6 convolution_convert_fusion
  442.0 17.8 %all_gather.16 = bf16[320,1024]{1,0:T(8,128)(2,1)S(1)} all-gather(bf16[160,1024]{1,0:T(8,128)(2,1)S(1)} %copy-done.8), channel_id=1, replica_groups=mesh['dp'=16,'mlp'=2] {'mlp'}, dimensions={0}, use_global_device_ids=true | all-gather | bytes 983040 | tf_op jit(solution)/shard_map/all_gather | solution.py:160
  459.8 5.7 multiply_convert_fusion
  469.1 9.4 %all-gather = bf16[1,1,320,1024]{3,2,1,0:T(8,128)(2,1)S(1)} all-gather(bf16[1,1,160,1024]{3,2,1,0:T(8,128)(2,1)S(1)} %copy-done.11), channel_id=2, replica_groups=mesh['dp'=16,'mlp'=2] {'mlp'}, dimensions={2}, use_global_device_ids=true | all-gather | bytes 983040 | tf_op jit(solution)/shard_map/all_gather | solution.py:176
  478.5 6.4 fusion.68
  488.6 6.1 convolution_convert_fusion.2
  494.7 4.4 convolution_convert_fusion.1
  499.1 49.8 %reduce-scatter.12.cloned.1.call-done = bf16[1024,1536]{1,0:T(8,128)(2,1)} async-done(((bf16[1024,3072]{1,0:T(8,128)(2,1)}), bf16[1024,1536]{1,0:T(8,128)(2,1)}) %reduce-scatter.12.cloned.1.call-update) | async-done | bytes 3145744 | tf_op jit(solution)/shard_map/reduce_scatter | solution.py:266
  551.5 16.2 %reduce-scatter.6.cloned.1.call-done = bf16[160,1024]{1,0:T(8,128)(2,1)} async-done(((bf16[320,1024]{1,0:T(8,128)(2,1)}), bf16[160,1024]{1,0:T(8,128)(2,1)}) %reduce-scatter.6.cloned.1.call-update) | async-done | bytes 327696 | tf_op jit(solution)/shard_map/reduce_scatter | solution.py:164
  570.4 15.7 %reduce-scatter.10.cloned.1.call-done = bf16[160,1024]{1,0:T(8,128)(2,1)} async-done(((bf16[320,1024]{1,0:T(8,128)(2,1)}), bf16[160,1024]{1,0:T(8,128)(2,1)}) %reduce-scatter.10.cloned.1.call-update) | async-done | bytes 327696 | tf_op jit(solution)/shard_map/reduce_scatter | solution.py:182
  586.1 6.1 fusion.53
  592.2 6.9 all-reduce.6
  599.4 63.3 %all-reduce.4 = (bf16[512]{0:T(512)(128)(2,1)S(1)}, bf16[512]{0:T(512)(128)(2,1)S(1)}, bf16[1536]{0:T(1024)(128)(2,1)S(1)}, bf16[512]{0:T(512)(128)(2,1)S(1)}, bf16[2048]{0:T(1024)(128)(2,1)S(1)}) all-reduce(bf16[512]{0:T(512)(128)(2,1)S(1)} %dynamic-slice.2, ...), channel_id=1, replica_groups=mesh['dp'=16,'mlp'=2] {'dp'}, use_global_device_ids=true, to_apply=%region_16.17 | all-reduce | flops 5120 | bytes 20480 | tf_op jit(solution)/shard_map/psum | solution.py:290
  667.2 157.0 %all-reduce.9.cloned.1.call-done = (bf16[1024,1536]{1,0:T(8,128)(2,1)}, bf16[1024,512]{1,0:T(8,128)(2,1)}, bf16[1024,2048]{1,0:T(8,128)(2,1)}, bf16[2048,1024]{1,0:T(8,128)(2,1)}) async-done(((bf16[1024,1536]{1,0:T(8,128)(2,1)}, bf16[1024,512]{1,0:T(8,128)(2,1)}, bf16[1024,2048]{1,0:T(8,128)(2,1)}, bf16[2048,1024]{1,0:T(8,128)(2,1)}), (bf16[1024,1536]{1,0:T(8,128)(2,1)}, bf16[1024,512]{1,0:T(8,128)(2,1)}, ...) | async-done | bytes 12582928 | tf_op jit(solution)/shard_map/psum | solution.py:286
  824.2 6.8 convert_element_type.175
  831.0 4.4 convert_element_type.178
  835.5 3.6 convert_element_type.169
  (187 shorter events, 82.1 us)
Async XLA Ops:
  7.2 188.6 %copy-start = (bf16[1024,1024]{1,0:T(8,128)(2,1)S(1)}, bf16[1024,1024]{1,0:T(8,128)(2,1)}, u32[]{:S(2)}) copy-start(bf16[1024,1024]{1,0:T(8,128)(2,1)} %param.23) | copy-start | bytes 6291460
  7.2 83.2 %all-gather.6.cloned.1.call-start = ((), (), s32[]{:S(2)}) async-start(), calls=%async_computation.6 | async-start | bytes 5570560 | tf_op jit(solution)/shard_map/all_gather | solution.py:121
  10.2 15.1 %copy-start.17 = (f32[160,8]{1,0:T(8,128)}, f32[160,8]{1,0:T(8,128)S(1)}, u32[]{:S(2)}) copy-start(f32[160,8]{1,0:T(8,128)S(1)} %copy.82) | copy-start | bytes 15364
  12.0 1.2 copy-start.26
  15.1 4.1 copy-start.7
  19.2 1.5 copy-start.9
  23.5 1.7 copy-start.5
  31.8 115.8 %all-gather.4.cloned.1.call-start = ((), (), s32[]{:S(2)}) async-start(), calls=%async_computation.5 | async-start | bytes 5570560 | tf_op jit(solution)/shard_map/all_gather | solution.py:122
  33.8 4.3 copy-start.32
  33.8 394.0 %reduce-scatter.8.cloned.1.call-start = ((), (), s32[]{:S(2)}) async-start(), calls=%async_computation.8 | async-start | bytes 11141120 | tf_op jit(solution)/shard_map/reduce_scatter | solution.py:243
  155.5 40.2 %copy-start.10 = (bf16[1,1,160,1024]{3,2,1,0:T(8,128)(2,1)S(1)}, bf16[1,1,160,1024]{3,2,1,0:T(8,128)(2,1)}, u32[]{:S(2)}) copy-start(bf16[1,1,160,1024]{3,2,1,0:T(8,128)(2,1)} %param.29) | copy-start | bytes 983044
  203.2 6.6 copy-start.3
  220.0 3.3 copy-start.1
  220.1 7.1 copy-start.2
  258.4 6.6 copy-start.3
  275.2 3.3 copy-start.1
  275.2 7.1 copy-start.2
  309.5 1.0 copy-start.11
  309.5 5.7 copy-start.4
  309.5 189.6 %reduce-scatter.14.cloned.1.call-start = ((), (), s32[]{:S(2)}) async-start(), calls=%async_computation.11 | async-start | bytes 3145728 | tf_op jit(solution)/shard_map/reduce_scatter | solution.py:269
  313.5 4.2 copy-start.18
  313.5 235.4 %reduce-scatter.12.cloned.1.call-start = ((), (), s32[]{:S(2)}) async-start(), calls=%async_computation.10 | async-start | bytes 9437184 | tf_op jit(solution)/shard_map/reduce_scatter | solution.py:266
  317.7 6.9 copy-start.16
  432.5 3.8 copy-start.8
  432.5 3.8 copy-start.14
  441.9 17.9 %copy-start.35 = (f32[2048]{0:T(1024)S(1)}, f32[2048]{0:T(1024)}, u32[]{:S(2)}) copy-start(f32[2048]{0:T(1024)} %param.26) | copy-start | bytes 24580
  441.9 125.8 %reduce-scatter.6.cloned.1.call-start = ((), (), s32[]{:S(2)}) async-start(), calls=%async_computation.7 | async-start | bytes 983040 | tf_op jit(solution)/shard_map/reduce_scatter | solution.py:164
  459.8 5.7 copy-start.21
  459.8 6.8 copy-start.33
  465.6 1.1 copy-start.37
  469.1 117.0 %reduce-scatter.10.cloned.1.call-start = ((), (), s32[]{:S(2)}) async-start(), calls=%async_computation.9 | async-start | bytes 983040 | tf_op jit(solution)/shard_map/reduce_scatter | solution.py:182
  478.5 6.5 copy-start.22
  478.5 7.5 copy-start.34
  485.0 1.1 copy-start.39
  488.5 335.7 %all-reduce.9.cloned.1.call-start = ((), (), s32[]{:S(2)}) async-start(), calls=%async_computation.12 | async-start | bytes 25165824 | tf_op jit(solution)/shard_map/psum | solution.py:286
  488.6 6.1 copy-start.23
  488.6 6.1 copy-start.38
  548.9 18.8 %copy-start.6 = (bf16[1,1,160,1024]{3,2,1,0:T(8,128)(2,1)S(1)}, bf16[1,1,160,1024]{3,2,1,0:T(8,128)(2,1)}, u32[]{:S(2)}) copy-start(bf16[1,1,160,1024]{3,2,1,0:T(8,128)(2,1)} %param.17) | copy-start | bytes 983044
  548.9 18.8 %copy-start.24 = (f32[1024]{0:T(1024)S(1)}, f32[1024]{0:T(1024)}, u32[]{:S(2)}) copy-start(f32[1024]{0:T(1024)} %param.28) | copy-start | bytes 12292
  548.9 18.8 %copy-start.25 = (f32[1024]{0:T(1024)S(1)}, f32[1024]{0:T(1024)}, u32[]{:S(2)}) copy-start(f32[1024]{0:T(1024)} %param.24) | copy-start | bytes 12292
  549.0 37.1 %copy-start.27 = (f32[160]{0:T(256)S(1)}, f32[160]{0:T(256)}, u32[]{:S(2)}) copy-start(f32[160]{0:T(256)} %copy-done.26) | copy-start | bytes 1924
  549.0 37.1 %copy-start.28 = (f32[1024]{0:T(1024)S(1)}, f32[1024]{0:T(1024)}, u32[]{:S(2)}) copy-start(f32[1024]{0:T(1024)} %param.19) | copy-start | bytes 12292
  549.0 37.1 %copy-start.30 = (f32[160]{0:T(256)S(1)}, f32[160]{0:T(256)}, u32[]{:S(2)}) copy-start(f32[160]{0:T(256)} %copy-done.29) | copy-start | bytes 1924
  567.7 2.5 copy-start.15
  663.9 176.8 %copy-start.31 = (f32[512]{0:T(512)}, f32[512]{0:T(512)S(1)}, u32[]{:S(2)}) copy-start(f32[512]{0:T(512)S(1)} %convert_element_type.173) | copy-start | bytes 6148
  824.2 6.8 copy-start.12
  831.0 4.4 copy-start.13
  835.5 3.6 copy-start.19
  (3 other events, 2.1 us)
Sparse Core Ops, SparseCore 0:
  31.9 58.4 all-gather.5
  93.3 54.3 all-gather.3
  309.6 118.0 reduce-scatter.7
  430.4 38.5 reduce-scatter.13
  471.8 77.1 reduce-scatter.11
  551.6 16.0 reduce-scatter.5
  570.0 16.0 reduce-scatter.9
  591.2 232.9 all-reduce.8
where the time goes:
time: 855 us; the launch traced here: 849 us
  waiting for transfers between devices  442 us (52%)
  matrix products  139 us (16%)
  local copies, waits for them, and re-layouts  107 us (13%)
  blocking collectives  97.4 us (11%)
  other arithmetic  44.8 us (5%)
  between operations  17 us (2%)
    psum x1, waiting for transfers between devices, local(): lax.psum(part_qkv.astype(jnp.bfloat16), 'dp').astype(jnp.float32)  157 us
    reduce_scatter x1, waiting for transfers between devices, local(): lax.psum_scatter(grad_kv_sum.astype(jnp.bfloat16), 'dp', scatter_dimensio...  101 us
    psum x1, blocking collectives, local(): lax.psum(part_gain.astype(jnp.bfloat16), 'dp').astype(jnp.float32)  63.3 us
    all_gather x1, waiting for transfers between devices, local(): keys_piece = lax.all_gather(keys_flat, 'dp', axis=0, tiled=True)  52.1 us
    reduce_scatter x1, waiting for transfers between devices, local(): lax.psum_scatter(grad_w_qkv.astype(jnp.bfloat16), 'mlp', scatter_dimensio...  49.8 us
    all_gather x1, waiting for transfers between devices, local(): values_piece = lax.all_gather(values_flat, 'dp', axis=0, tiled=True)  49.4 us
    dynamic_update_slice x4, local copies, waits for them, and re-layouts, local(): lax.scan(back_one_block, grad_query_sum, (keys_piece.reshape(blocks, back...  27.2 us
    unnamed x83, local copies, waits for them, and re-layouts  23 us
  transfers between devices with their start and end apart: 8, of which 7 were waited for; matrix products, arithmetic and copies ran while one was open for 10% of the time, Pallas kernels for 0%

commit v1 on v0

--- a/solution.py
+++ b/solution.py
@@ -11,6 +11,13 @@
 ROPE_BASE = 10000.0
 SQRT_HALF = 1.0 / math.sqrt(2.0)
 INV_ROOT_TWO_PI = 1.0 / math.sqrt(2.0 * math.pi)
+
+
+def plan_packet_all(work_x, frame_in):
+    high = jnp.concatenate([frame_in, work_x], axis=1)
+    y_new = jax.lax.all_gather(high, axis_name="dp", axis=0, tiled=True)
+    oldest = jnp.split(y_new, [frame_in.shape[1]], axis=1)
+    return oldest
 
 
 def rotate(values, positions, sign_factor):
@@ -118,8 +125,7 @@
         jnp.zeros((tok_count, HEADS, HEAD_DIM), jnp.float32),
         jnp.zeros((HEADS, tok_count), jnp.float32),
     )
-    keys_piece = lax.all_gather(keys_flat, "dp", axis=0, tiled=True)
-    values_piece = lax.all_gather(values_flat, "dp", axis=0, tiled=True)
+    keys_piece, values_piece = plan_packet_all(values_flat, keys_flat)
     piece_rows = keys_piece.shape[0]
     blocks = piece_count(piece_rows)
     sub_rows = piece_rows // blocks

time: 855 us -> 915 us (1.070)
  local copies, waits for them, and re-layouts: 107 us -> 129 us
  waiting for transfers between devices: 442 us -> 461 us
  matrix products: 139 us -> 157 us
    all_gather x0 -> x1, waiting for transfers between devices: none -> 84.7 us  [plan_packet_all(): y_new = jax.lax.all_gather(high, axis_name='dp', axis=0, tiled=True)]
    all_gather x1, waiting for transfers between devices: 52.1 us -> 0.02 us  [local(): keys_piece = lax.all_gather(keys_flat, 'dp', axis=0, tiled=True)]
    dynamic_slice x8 -> x16, local copies, waits for them, and re-layouts: 17.6 us -> 57.1 us  [local(): lax.scan(attend_one_block, start_state, (keys_piece.reshape(blocks, sub_r...]
    unnamed x83 -> x79, local copies, waits for them, and re-layouts: 23 us -> 6.82 us
    all_gather x1, waiting for transfers between devices: 49.4 us -> 34.3 us  [local(): values_piece = lax.all_gather(values_flat, 'dp', axis=0, tiled=True)]
    split x0 -> x1, local copies, waits for them, and re-layouts: none -> 9.39 us  [plan_packet_all(): oldest = jnp.split(y_new, [frame_in.shape[1]], axis=1)]
  transfers between devices with their start and end apart: 8 -> 9, of which waited for: 7 -> 7; matrix products, arithmetic and copies ran while one was open for 10% -> 17% of each run, Pallas kernels for 0% -> 0%
where the time goes in v1:
time: 915 us; the launch traced here: 909 us
  waiting for transfers between devices  461 us (50%)
  matrix products  157 us (17%)
  local copies, waits for them, and re-layouts  129 us (14%)
  blocking collectives  97.1 us (11%)
  other arithmetic  46.8 us (5%)
  between operations  16.5 us (2%)
    psum x1, waiting for transfers between devices, local(): lax.psum(part_qkv.astype(jnp.bfloat16), 'dp').astype(jnp.float32)  157 us
    reduce_scatter x1, waiting for transfers between devices, local(): lax.psum_scatter(grad_kv_sum.astype(jnp.bfloat16), 'dp', scatter_dimensio...  101 us
    all_gather x1, waiting for transfers between devices, plan_packet_all(): y_new = jax.lax.all_gather(high, axis_name='dp', axis=0, tiled=True)  84.7 us
    psum x1, blocking collectives, local(): lax.psum(part_gain.astype(jnp.bfloat16), 'dp').astype(jnp.float32)  63.1 us
    dynamic_slice x16, local copies, waits for them, and re-layouts, local(): lax.scan(attend_one_block, start_state, (keys_piece.reshape(blocks, sub_r...  57.1 us
    reduce_scatter x1, waiting for transfers between devices, local(): lax.psum_scatter(grad_w_qkv.astype(jnp.bfloat16), 'mlp', scatter_dimensio...  49.8 us
    all_gather x1, waiting for transfers between devices, local(): values_piece = lax.all_gather(values_flat, 'dp', axis=0, tiled=True)  34.3 us
    dynamic_update_slice x4, local copies, waits for them, and re-layouts, local(): lax.scan(back_one_block, grad_query_sum, (keys_piece.reshape(blocks, back...  27.1 us
  transfers between devices with their start and end apart: 9, of which 7 were waited for; matrix products, arithmetic and copies ran while one was open for 17% of the time, Pallas kernels for 0%

profile of v1, /device:TPU:0, one launch (start us, length us, event | category | flops | bytes accessed | tf_op | source)
XLA Modules:
  0.0 908.5 jit_solution(14349169153219333106)
XLA Ops:
  39.0 84.7 %all-gather.5.cloned.1.call-done = bf16[2560,2048]{1,0:T(8,128)(2,1)} async-done(((bf16[160,2048]{1,0:T(8,128)(2,1)}), bf16[2560,2048]{1,0:T(8,128)(2,1)}) %all-gather.5.cloned.1.call-update) | async-done | bytes 10485776 | tf_op jit(solution)/shard_map/all_gather | solution.py:18
  123.7 9.4 %fusion.66 = (bf16[2560,1024]{1,0:T(8,128)(2,1)}, bf16[2560,1024]{1,0:T(8,128)(2,1)}) fusion(bf16[2560,2048]{1,0:T(8,128)(2,1)} %all-gather.5.cloned.1.call-done), kind=kLoop, calls=%fused_computation.135 | loop fusion | bytes 20971520 | tf_op jit(solution)/shard_map/split | solution.py:19
  133.1 66.9 %while.26 = (s32[]{:T(128)}, f32[160,16,64]{0,2,1:T(8,128)}, f32[16,160]{1,0:T(8,128)S(1)}, bf16[2,1280,1024]{2,1,0:T(8,128)(2,1)}, s32[2,1280]{1,0:T(2,128)S(1)...) while((s32[]{:T(128)}, f32[160,16,64]{0,2,1:T(8,128)}, ...), condition=%wide.region_5.6_spmd.clone, body=%wide.region_3.5_spmd.clone.sunk | while | flops 859056768 | bytes 54739320 | solution.py:153
  133.1 5.5 constant_dynamic-slice_fusion.6
  138.6 4.4 copy.119
  143.2 10.0 %fusion.125 = (f32[16,160]{1,0:T(8,128)S(1)}, f32[16,1280,160]{1,2,0:T(8,128)}) fusion(pred[160,1280]{1,0:T(8,128)(4,1)S(1)} %broadcast_compare_fusion.4, bf16[1280,16,64]{0,2,1:T(8,128)(2,1)} %bitcast.211, bf16[160,16,64]{0,2,1:T(8,128)(2,1)S(1)} %get-tuple-element.522), kind=kOutput, calls=%fused_computation.3.clone.1 | convolution fusion | flops 429258240 | bytes 16271360 | tf_op jit(solution)/shard_map/while/body/eval_jaxpr/qhd,khd->hqk/dot_general | solution.py:139
  153.2 4.4 copy.118
  157.6 9.0 fusion.126
  166.5 5.4 constant_dynamic-slice_fusion.6
  172.0 4.4 copy.119
  176.6 9.8 %fusion.125 = (f32[16,160]{1,0:T(8,128)S(1)}, f32[16,1280,160]{1,2,0:T(8,128)}) fusion(pred[160,1280]{1,0:T(8,128)(4,1)S(1)} %broadcast_compare_fusion.4, bf16[1280,16,64]{0,2,1:T(8,128)(2,1)} %bitcast.211, bf16[160,16,64]{0,2,1:T(8,128)(2,1)S(1)} %get-tuple-element.522), kind=kOutput, calls=%fused_computation.3.clone.1 | convolution fusion | flops 429258240 | bytes 16271360 | tf_op jit(solution)/shard_map/while/body/eval_jaxpr/qhd,khd->hqk/dot_general | solution.py:139
  186.5 4.4 copy.118
  190.9 9.1 %fusion.126 = f32[160,16,64]{0,2,1:T(8,128)} fusion(bf16[1280,16,64]{0,2,1:T(8,128)(2,1)} %bitcast.212, f32[16,1280,160]{1,2,0:T(8,128)} %get-tuple-element.482, pred[160,1280]{1,0:T(8,128)(4,1)S(1)} %broadcast_compare_fusion.4, f32[160,16,64]{0,2,1:T(8,128)} %get-tuple-element.507, pred[]{:T(512)S(6)} %compare.6), kind=kOutput, calls=%fused_computation.10.clone.1 | convolution fusion | flops 429588480 | bytes 17244160 | tf_op jit(solution)/shard_map/while/body/eval_jaxpr/hqk,khd->qhd/dot_general | solution.py:145
  203.0 34.3 %all-gather.9.cloned.1.call-done = bf16[2560,1024]{1,0:T(8,128)(2,1)} async-done(((bf16[160,1024]{1,0:T(8,128)(2,1)}), bf16[2560,1024]{1,0:T(8,128)(2,1)}) %all-gather.9.cloned.1.call-update) | async-done | bytes 5242896 | tf_op jit(solution)/shard_map/all_gather | solution.py:198
  237.2 132.6 %while.27 = (s32[]{:T(128)}, f32[160,16,64]{0,2,1:T(8,128)}, bf16[2,1280,2048]{2,1,0:T(8,128)(2,1)}, bf16[2,1280,1024]{2,1,0:T(8,128)(2,1)}, s32[2,1280]{1,0:T(2...) while((s32[]{:T(128)}, f32[160,16,64]{0,2,1:T(8,128)}, ...), condition=%wide.region_9.10_spmd.clone, body=%wide.region_8.9_spmd.clone.sunk | while | flops 2137170048 | bytes 155306960 | solution.py:239
  237.4 5.5 constant_dynamic-slice_fusion.7
  242.9 4.4 copy.120
  247.3 8.3 fusion.137
  260.2 9.9 %fusion.138 = bf16[16,160,1280]{2,1,0:T(8,128)(2,1)S(1)} fusion(f32[16,1280,160]{1,2,0:T(8,128)} %fusion.137, bf16[1280,16,64]{0,2,1:T(8,128)(2,1)} %bitcast.213, bf16[160,16,64]{0,2,1:T(8,128)(2,1)} %get-tuple-element.557, f32[16,160]{1,0:T(8,128)S(1)} %bitcast.223, pred[160,1280]{1,0:T(8,128)(4,1)S(1)} %broadcast_compare_fusion.5), kind=kOutput, calls=%fused_computation.20.clone.1 | convolution fusion | flops 435814400 | bytes 22824960 | tf_op jit(solution)/shard_map/while/body/eval_jaxpr/qhd,khd->hqk/dot_general | solution.py:214
  273.0 7.2 fusion.140
  282.9 7.9 copy.122
  290.8 5.6 constant_dynamic-update-slice_fusion.2
  296.4 6.9 fusion.139
  303.3 5.5 constant_dynamic-slice_fusion.7
  308.8 4.4 copy.120
  313.2 8.3 fusion.137
  326.1 9.9 %fusion.138 = bf16[16,160,1280]{2,1,0:T(8,128)(2,1)S(1)} fusion(f32[16,1280,160]{1,2,0:T(8,128)} %fusion.137, bf16[1280,16,64]{0,2,1:T(8,128)(2,1)} %bitcast.213, bf16[160,16,64]{0,2,1:T(8,128)(2,1)} %get-tuple-element.557, f32[16,160]{1,0:T(8,128)S(1)} %bitcast.223, pred[160,1280]{1,0:T(8,128)(4,1)S(1)} %broadcast_compare_fusion.5), kind=kOutput, calls=%fused_computation.20.clone.1 | convolution fusion | flops 435814400 | bytes 22824960 | tf_op jit(solution)/shard_map/while/body/eval_jaxpr/qhd,khd->hqk/dot_general | solution.py:214
  338.9 7.2 fusion.140
  348.8 7.9 copy.122
  356.7 5.7 constant_dynamic-update-slice_fusion.2
  362.4 7.1 fusion.139
  386.7 101.4 %reduce-scatter.8.cloned.1.call-done = bf16[160,2048]{1,0:T(8,128)(2,1)} async-done(((bf16[2560,2048]{1,0:T(8,128)(2,1)}), bf16[160,2048]{1,0:T(8,128)(2,1)}) %reduce-scatter.8.cloned.1.call-update) | async-done | bytes 655376 | tf_op jit(solution)/shard_map/reduce_scatter | solution.py:249
  496.7 5.6 convolution_convert_fusion
  502.3 17.8 %all_gather.16 = bf16[320,1024]{1,0:T(8,128)(2,1)S(1)} all-gather(bf16[160,1024]{1,0:T(8,128)(2,1)S(1)} %copy-done.7), channel_id=1, replica_groups=mesh['dp'=16,'mlp'=2] {'mlp'}, dimensions={0}, use_global_device_ids=true | all-gather | bytes 983040 | tf_op jit(solution)/shard_map/all_gather | solution.py:166
  520.2 5.7 multiply_convert_fusion
  529.5 9.2 %all-gather = bf16[1,1,320,1024]{3,2,1,0:T(8,128)(2,1)S(1)} all-gather(bf16[1,1,160,1024]{3,2,1,0:T(8,128)(2,1)S(1)} %copy-done.9), channel_id=2, replica_groups=mesh['dp'=16,'mlp'=2] {'mlp'}, dimensions={2}, use_global_device_ids=true | all-gather | bytes 983040 | tf_op jit(solution)/shard_map/all_gather | solution.py:182
  538.6 6.7 fusion.69
  549.0 6.1 convolution_convert_fusion.2
  555.1 4.4 convolution_convert_fusion.1
  559.5 49.8 %reduce-scatter.12.cloned.1.call-done = bf16[1024,1536]{1,0:T(8,128)(2,1)} async-done(((bf16[1024,3072]{1,0:T(8,128)(2,1)}), bf16[1024,1536]{1,0:T(8,128)(2,1)}) %reduce-scatter.12.cloned.1.call-update) | async-done | bytes 3145744 | tf_op jit(solution)/shard_map/reduce_scatter | solution.py:272
  611.8 16.4 %reduce-scatter.6.cloned.1.call-done = bf16[160,1024]{1,0:T(8,128)(2,1)} async-done(((bf16[320,1024]{1,0:T(8,128)(2,1)}), bf16[160,1024]{1,0:T(8,128)(2,1)}) %reduce-scatter.6.cloned.1.call-update) | async-done | bytes 327696 | tf_op jit(solution)/shard_map/reduce_scatter | solution.py:170
  630.9 15.7 %reduce-scatter.10.cloned.1.call-done = bf16[160,1024]{1,0:T(8,128)(2,1)} async-done(((bf16[320,1024]{1,0:T(8,128)(2,1)}), bf16[160,1024]{1,0:T(8,128)(2,1)}) %reduce-scatter.10.cloned.1.call-update) | async-done | bytes 327696 | tf_op jit(solution)/shard_map/reduce_scatter | solution.py:188
  646.6 6.1 fusion.53
  652.6 6.9 all-reduce.6
  659.9 63.1 %all-reduce.4 = (bf16[512]{0:T(512)(128)(2,1)S(1)}, bf16[512]{0:T(512)(128)(2,1)S(1)}, bf16[1536]{0:T(1024)(128)(2,1)S(1)}, bf16[512]{0:T(512)(128)(2,1)S(1)}, bf16[2048]{0:T(1024)(128)(2,1)S(1)}) all-reduce(bf16[512]{0:T(512)(128)(2,1)S(1)} %dynamic-slice.2, ...), channel_id=1, replica_groups=mesh['dp'=16,'mlp'=2] {'dp'}, use_global_device_ids=true, to_apply=%region_16.17 | all-reduce | flops 5120 | bytes 20480 | tf_op jit(solution)/shard_map/psum | solution.py:296
  727.6 157.1 %all-reduce.9.cloned.1.call-done = (bf16[1024,1536]{1,0:T(8,128)(2,1)}, bf16[1024,512]{1,0:T(8,128)(2,1)}, bf16[1024,2048]{1,0:T(8,128)(2,1)}, bf16[2048,1024]{1,0:T(8,128)(2,1)}) async-done(((bf16[1024,1536]{1,0:T(8,128)(2,1)}, bf16[1024,512]{1,0:T(8,128)(2,1)}, bf16[1024,2048]{1,0:T(8,128)(2,1)}, bf16[2048,1024]{1,0:T(8,128)(2,1)}), (bf16[1024,1536]{1,0:T(8,128)(2,1)}, bf16[1024,512]{1,0:T(8,128)(2,1)}, ...) | async-done | bytes 12582928 | tf_op jit(solution)/shard_map/psum | solution.py:292
  884.7 6.8 convert_element_type.175
  891.5 4.4 convert_element_type.178
  (192 shorter events, 101.3 us)
Async XLA Ops:
  7.2 192.8 %copy-start = (bf16[1024,1024]{1,0:T(8,128)(2,1)S(1)}, bf16[1024,1024]{1,0:T(8,128)(2,1)}, u32[]{:S(2)}) copy-start(bf16[1024,1024]{1,0:T(8,128)(2,1)} %param.23) | copy-start | bytes 6291460
  7.2 116.5 %all-gather.5.cloned.1.call-start = ((), (), s32[]{:S(2)}) async-start(), calls=%async_computation.5 | async-start | bytes 11141120 | tf_op jit(solution)/shard_map/all_gather | solution.py:18
  8.5 1.2 copy-start.24
  11.6 4.1 copy-start.6
  15.7 1.7 copy-start.30
  19.5 5.3 copy-start.15
  23.1 1.7 copy-start.3
  33.3 169.6 %all-gather.7.cloned.1.call-start = ((), (), s32[]{:S(2)}) async-start(), calls=%async_computation.7 | async-start | bytes 5570560 | tf_op jit(solution)/shard_map/all_gather | solution.py:197
  34.1 203.2 %all-gather.9.cloned.1.call-start = ((), (), s32[]{:S(2)}) async-start(), calls=%async_computation.8 | async-start | bytes 5570560 | tf_op jit(solution)/shard_map/all_gather | solution.py:198
  34.8 453.4 %reduce-scatter.8.cloned.1.call-start = ((), (), s32[]{:S(2)}) async-start(), calls=%async_computation.9 | async-start | bytes 11141120 | tf_op jit(solution)/shard_map/reduce_scatter | solution.py:249
  133.1 66.9 %copy-start.8 = (bf16[1,1,160,1024]{3,2,1,0:T(8,128)(2,1)S(1)}, bf16[1,1,160,1024]{3,2,1,0:T(8,128)(2,1)}, u32[]{:S(2)}) copy-start(bf16[1,1,160,1024]{3,2,1,0:T(8,128)(2,1)} %param.29) | copy-start | bytes 983044
  270.2 2.8 copy-start.1
  270.2 2.8 copy-start.4
  336.1 2.8 copy-start.1
  336.1 2.8 copy-start.4
  369.9 1.0 copy-start.9
  369.9 5.5 copy-start.2
  369.9 189.5 %reduce-scatter.14.cloned.1.call-start = ((), (), s32[]{:S(2)}) async-start(), calls=%async_computation.12 | async-start | bytes 3145728 | tf_op jit(solution)/shard_map/reduce_scatter | solution.py:275
  373.9 4.0 copy-start.16
  373.9 235.3 %reduce-scatter.12.cloned.1.call-start = ((), (), s32[]{:S(2)}) async-start(), calls=%async_computation.11 | async-start | bytes 9437184 | tf_op jit(solution)/shard_map/reduce_scatter | solution.py:272
  377.9 6.9 copy-start.14
  491.4 0.9 copy-start.18
  492.9 3.8 copy-start.7
  492.9 3.8 copy-start.12
  502.3 17.9 %copy-start.33 = (f32[2048]{0:T(1024)S(1)}, f32[2048]{0:T(1024)}, u32[]{:S(2)}) copy-start(f32[2048]{0:T(1024)} %param.26) | copy-start | bytes 24580
  502.3 125.9 %reduce-scatter.6.cloned.1.call-start = ((), (), s32[]{:S(2)}) async-start(), calls=%async_computation.6 | async-start | bytes 983040 | tf_op jit(solution)/shard_map/reduce_scatter | solution.py:170
  520.2 5.7 copy-start.19
  520.2 6.8 copy-start.31
  525.9 1.1 copy-start.35
  529.4 117.2 %reduce-scatter.10.cloned.1.call-start = ((), (), s32[]{:S(2)}) async-start(), calls=%async_computation.10 | async-start | bytes 983040 | tf_op jit(solution)/shard_map/reduce_scatter | solution.py:188
  538.6 6.7 copy-start.20
  538.6 7.8 copy-start.32
  545.4 1.1 copy-start.37
  548.9 335.8 %all-reduce.9.cloned.1.call-start = ((), (), s32[]{:S(2)}) async-start(), calls=%async_computation.13 | async-start | bytes 25165824 | tf_op jit(solution)/shard_map/psum | solution.py:292
  548.9 6.1 copy-start.21
  549.0 6.1 copy-start.36
  609.3 0.7 copy-start.34
  609.3 18.9 %copy-start.5 = (bf16[1,1,160,1024]{3,2,1,0:T(8,128)(2,1)S(1)}, bf16[1,1,160,1024]{3,2,1,0:T(8,128)(2,1)}, u32[]{:S(2)}) copy-start(bf16[1,1,160,1024]{3,2,1,0:T(8,128)(2,1)} %param.17) | copy-start | bytes 983044
  609.3 18.9 %copy-start.22 = (f32[1024]{0:T(1024)S(1)}, f32[1024]{0:T(1024)}, u32[]{:S(2)}) copy-start(f32[1024]{0:T(1024)} %param.28) | copy-start | bytes 12292
  609.3 18.9 %copy-start.23 = (f32[1024]{0:T(1024)S(1)}, f32[1024]{0:T(1024)}, u32[]{:S(2)}) copy-start(f32[1024]{0:T(1024)} %param.24) | copy-start | bytes 12292
  609.3 37.2 %copy-start.25 = (f32[160]{0:T(256)S(1)}, f32[160]{0:T(256)}, u32[]{:S(2)}) copy-start(f32[160]{0:T(256)} %copy-done.24) | copy-start | bytes 1924
  609.4 37.2 %copy-start.26 = (f32[1024]{0:T(1024)S(1)}, f32[1024]{0:T(1024)}, u32[]{:S(2)}) copy-start(f32[1024]{0:T(1024)} %param.19) | copy-start | bytes 12292
  609.4 37.2 %copy-start.28 = (f32[160]{0:T(256)S(1)}, f32[160]{0:T(256)}, u32[]{:S(2)}) copy-start(f32[160]{0:T(256)} %copy-done.27) | copy-start | bytes 1924
  628.2 2.5 copy-start.13
  724.2 176.9 %copy-start.29 = (f32[512]{0:T(512)}, f32[512]{0:T(512)S(1)}, u32[]{:S(2)}) copy-start(f32[512]{0:T(512)S(1)} %convert_element_type.173) | copy-start | bytes 6148
  884.7 6.8 copy-start.10
  891.5 4.4 copy-start.11
  896.0 3.6 copy-start.17
  (1 other events, 0.6 us)
Sparse Core Ops, SparseCore 0:
  33.4 90.2 all-gather.4
  126.0 53.9 all-gather.6
  182.9 54.3 all-gather.8
  370.0 118.0 reduce-scatter.7
  490.8 38.5 reduce-scatter.13
  532.1 77.1 reduce-scatter.11
  612.1 16.0 reduce-scatter.5
  630.5 16.0 reduce-scatter.9
  651.7 232.9 all-reduce.8
